TPU v7x, 256 devices: a whole 4x4x8 slice. The times are simulated.
256 devices in a mesh: node: 32 (over z, x), local: 8 (over y, core).
Axes of the slice: x: 4, y: 4, z: 8, core: 2. Of those that a mesh axis runs over, the one named last changes fastest.
Arguments:
- gate_pre: bfloat16 [14336, 15360], P('node', 'local'), may hold values from -6 to 6
- up_pre: bfloat16 [14336, 15360], P('node', 'local'), may hold values from -6 to 6
- out_grad: bfloat16 [14336, 4096], P('node', 'local'), may hold values from -6 to 6
Outputs:
- weight_grad: float32 [15360, 4096], P('local', 'node')
All inputs are finite; a program needn't handle non-finite values.
Results may differ from a plain program's by a relative error of at most 0.015.
Values may be sent and summed in bfloat16 or wider, within the bound.
A program may use at most 128 MiB of HBM per device.

v0:
```python
import jax
import jax.numpy as jnp
from jax import lax
from jax.sharding import Mesh
from jax.sharding import PartitionSpec as P

NODE = ("node_0", "node_1")
LOCAL = ("local_0", "local_1")


def copy_for_each(value, axis):
    copies = jnp.broadcast_to(value, (lax.axis_size(axis), *value.shape))
    return lax.all_to_all(copies, axis, split_axis=0, concat_axis=0, tiled=True)


def joined_along(parts, dim):
    dims = list(parts.shape[1:])
    dims[dim] *= parts.shape[0]
    return jnp.moveaxis(parts, 0, dim).reshape(dims)


def whole_of(value, axes, dim):
    far, near = axes
    parts = copy_for_each(copy_for_each(value, far), near)
    return joined_along(parts.swapaxes(0, 1).reshape(-1, *value.shape), dim)


def sum_by_axis(terms, axes):
    running = terms.astype(jnp.bfloat16)
    for axis in axes:
        running = lax.psum_scatter(running, axis, scatter_dimension=0, tiled=True)
    return running.astype(jnp.float32)


def shards(gate_pre, up_pre, out_grad):
    gate_float = gate_pre.astype(jnp.float32)
    activated = gate_float * jax.nn.sigmoid(gate_float)
    hidden = (activated * up_pre.astype(jnp.float32)).astype(jnp.bfloat16)
    averaging = 1.0 / lax.axis_size(NODE)
    gathered = whole_of(out_grad, ("local_0", "local_1"), 1)
    transposed = sum_by_axis(
        lax.dot_general(
            gathered, hidden, (((0,), (0,)), ((), ())), preferred_element_type=jnp.float32
        )
        * averaging,
        NODE,
    )
    shard = transposed.T
    return shard


def solution(mesh):
    torus = Mesh(mesh.devices.reshape(8, 4, 4, 2), ("node_0", "node_1", "local_0", "local_1"))
    placed = (P(NODE, LOCAL), P(NODE, LOCAL), P(NODE, LOCAL))
    return jax.shard_map(
        shards, mesh=torus, in_specs=placed, out_specs=P(LOCAL, NODE), check_vma=False
    )
```

profile of v0, /device:TPU:1, one launch (start us, length us, event | category | flops | bytes accessed | tf_op | source)
XLA Modules:
  0.0 265.6 jit_solution(16719022184939676013)
XLA Ops:
  6.5 0.0 reduce-scatter.5.cloned.1.call-start
  6.5 1.2 broadcast_in_dim.6
  7.7 27.5 %all_to_all.10 = bf16[4,448,512]{2,1,0:T(8,128)(2,1)S(1)} all-to-all(bf16[4,448,512]{2,1,0:T(8,128)(2,1)S(1)} %broadcast_in_dim.6), channel_id=1, replica_groups=mesh['node_0'=8,'node_1'=4,'local_0'=4,'local_1'=2] {'local_0'}, dimensions={0} | all-to-all | bytes 3670016 | tf_op jit(solution)/shard_map/all_to_all | solution.py:13
  35.2 0.3 broadcast_in_dim.7
  35.5 8.1 %all_to_all.11 = bf16[2,4,448,512]{3,2,1,0:T(8,128)(2,1)S(1)} all-to-all(bf16[2,4,448,512]{3,2,1,0:T(8,128)(2,1)S(1)} %broadcast_in_dim.7), channel_id=1, replica_groups=mesh['node_0'=8,'node_1'=4,'local_0'=4,'local_1'=2] {'local_1'}, dimensions={0} | all-to-all | bytes 7340032 | tf_op jit(solution)/shard_map/all_to_all | solution.py:13
  43.6 0.2 copy.5
  43.8 0.0 copy-start
  43.9 0.0 copy-start.1
  43.9 0.5 copy.9
  44.4 0.9 copy-done
  45.3 0.5 copy-done.1
  45.8 11.6 %fusion = bf16[4096,1920]{0,1:T(8,128)(2,1)} fusion(bf16[448,4096]{1,0:T(8,128)(2,1)S(1)} %bitcast.14, bf16[448,1920]{1,0:T(8,128)(2,1)S(1)} %copy-done, bf16[448,1920]{1,0:T(8,128)(2,1)S(1)} %copy-done.1), kind=kOutput, calls=%fused_computation.1 | convolution fusion | flops 7069040640 | bytes 22839296 | tf_op jit(solution)/shard_map/dot_general | solution.py:42
  57.4 0.0 reduce-scatter.5.cloned.1.call-update
  57.5 0.0 reduce-scatter.7.cloned.1.call-start
  57.5 164.9 %reduce-scatter.5.cloned.1.call-done = bf16[512,1920]{0,1:T(8,128)(2,1)} async-done(((bf16[4096,1920]{0,1:T(8,128)(2,1)}), bf16[512,1920]{0,1:T(8,128)(2,1)}) %reduce-scatter.5.cloned.1.call-update) | async-done | bytes 1966096 | tf_op jit(solution)/shard_map/reduce_scatter | solution.py:31
  222.4 4.0 %copy.7 = bf16[512,1920]{1,0:T(8,128)(2,1)} copy(bf16[512,1920]{0,1:T(8,128)(2,1)} %reduce-scatter.5.cloned.1.call-done) | data formatting | bytes 3932160
  226.5 0.0 reduce-scatter.7.cloned.1.call-update
  226.5 29.9 %reduce-scatter.7.cloned.1.call-done = bf16[128,1920]{1,0:T(8,128)(2,1)} async-done(((bf16[512,1920]{1,0:T(8,128)(2,1)}), bf16[128,1920]{1,0:T(8,128)(2,1)}) %reduce-scatter.7.cloned.1.call-update) | async-done | bytes 491536
  256.4 1.3 copy.8
  257.7 1.0 convert_bitcast_fusion
Async XLA Ops:
  6.5 215.9 %reduce-scatter.5.cloned.1.call-start = ((), (), s32[]{:S(2)}) async-start(), calls=%async_computation.4 | async-start | bytes 17694720 | tf_op jit(solution)/shard_map/reduce_scatter | solution.py:31
  43.8 1.5 copy-start
  43.9 2.0 copy-start.1
  57.5 199.0 %reduce-scatter.7.cloned.1.call-start = ((), (), s32[]{:S(2)}) async-start(), calls=%async_computation.5 | async-start | bytes 2457600
Sparse Core Ops, SparseCore 0:
  57.6 164.8 reduce-scatter.4
  226.6 29.7 reduce-scatter.6
where the time goes:
time: 266 us
  waiting for transfers between devices  195 us (73%)
  blocking collectives  35.6 us (13%)
  between operations  13.5 us (5%)
  matrix products  11.6 us (4%)
  local copies, waits for them, and re-layouts  8.99 us (3%)
    reduce_scatter x1, waiting for transfers between devices, sum_by_axis(): running = lax.psum_scatter(running, axis, scatter_dimension=0, tiled=True)  165 us
    all_to_all x2, blocking collectives, copy_for_each(): return lax.all_to_all(copies, axis, split_axis=0, concat_axis=0, tiled=True)  35.6 us
    unnamed x3, waiting for transfers between devices  30 us
    dot_general x1, matrix products, shards(): lax.dot_general(gathered, hidden, (((0,), (0,)), ((), ())), preferred_ele...  11.6 us
    unnamed x6, local copies, waits for them, and re-layouts  6.77 us
  transfers between devices with their start and end apart: 2, of which 2 were waited for; matrix products, arithmetic and copies ran while one was open for 0% of the time, Pallas kernels for 0%

commit v1 on v0

v1 whole, which is shorter than its diff:
```python
import jax
import jax.numpy as jnp
from jax import lax
from jax.experimental import pallas as pl
from jax.experimental.pallas import tpu as pltpu
from jax.sharding import PartitionSpec as P

MESH = pl.DeviceIdType.MESH
NZ, NX, NY, NC = 8, 4, 4, 2
MC = 128
NB = 128
AHEAD = 5
LAG = 2


def kernel(
    gate_hbm, up_hbm, grad_hbm, out_hbm,
    gate_buf, up_buf, rows, turned, cols, prod, z_out, z_in, total,
    load_sem, own_sem, x_send, x_recv, bx_send, bx_recv, by_send, by_recv, bs_send, bs_recv,
    z_send, z_recv, out_sem,
):
    tokens = grad_hbm.shape[0]
    chunks = gate_hbm.shape[1] // MC
    node, local = lax.axis_index("node"), lax.axis_index("local")
    z, x = node // NX, node % NX
    y, core = local // NC, local % NC
    mine = y * NC + core

    def at(dz=0, dx=0, dy=0, dc=0):
        return {
            "node": lax.rem(z + dz + NZ, NZ) * NX + lax.rem(x + dx + NX, NX),
            "local": lax.rem(y + dy + NY, NY) * NC + lax.rem(core + dc, NC),
        }

    def remote(src, dst, send, recv, device):
        return pltpu.make_async_remote_copy(
            src_ref=src, dst_ref=dst, send_sem=send, recv_sem=recv, device_id=device, device_id_type=MESH
        )

    partners = (at(dz=1), at(dz=-1), at(dx=1), at(dx=-1), at(dx=2), at(dy=1), at(dy=-1), at(dc=1))
    barrier = pltpu.get_barrier_semaphore()
    for device in partners:
        pl.semaphore_signal(barrier, inc=1, device_id=device, device_id_type=MESH)

    def load(i):
        at_i = pl.ds(pl.multiple_of(i * MC, MC), MC)
        return (
            pltpu.make_async_copy(gate_hbm.at[:, at_i], gate_buf.at[i], load_sem.at[0, i]),
            pltpu.make_async_copy(up_hbm.at[:, at_i], up_buf.at[i], load_sem.at[1, i]),
        )

    def row_block(who):
        return pl.ds(pl.multiple_of(who * tokens, tokens), tokens)

    def lanes(block):
        return pl.ds(pl.multiple_of(block * NB, NB), NB)

    x_of = (x, lax.rem(x + NX - 1, NX), lax.rem(x + 1, NX), lax.rem(x + 2, NX))

    def piece(k, block):
        return cols.at[row_block(x_of[k]), lanes(block)]

    own_copy = pltpu.make_async_copy(grad_hbm.at[:, lanes(x)], piece(0, mine), own_sem)
    own_copy.start()
    for i in range(chunks):
        for copy in load(i):
            copy.start()

    pl.semaphore_wait(barrier, len(partners))

    def bx(k, dx):
        dest = lax.rem(x + dx + NX, NX)
        return remote(grad_hbm.at[:, lanes(dest)], piece(0, mine), bx_send.at[k], bx_recv.at[k], at(dx=dx))

    steps_x = ((0, 1), (1, -1), (2, 2))
    for k, dx in steps_x:
        bx(k, dx).start()

    def by(k, which, block, dy):
        return remote(piece(k, block), piece(k, block), by_send.at[k, which], by_recv.at[k, which], at(dy=dy))

    def bs(k, source, block):
        return remote(piece(k, block), piece(k, block), bs_send.at[k, source], bs_recv.at[k, source], at(dc=1))

    below = lax.rem(y + NY - 1, NY) * NC + core
    above = lax.rem(y + 1, NY) * NC + core
    across = lax.rem(y + 2, NY) * NC + core

    def spread(k):
        by(k, 0, mine, 1).start()
        by(k, 1, mine, -1).start()
        bs(k, 0, mine).start()

    def spread_on(k):
        flip = lax.rem(core + k, 2)
        by(k, 0, below, 1).wait_recv()
        by(k, 1, above, 1).wait_recv()
        passed = jnp.where(flip == 0, below, above)
        by(k, 2, passed, jnp.where(flip == 0, 1, -1)).start()
        bs(k, 1, below).start()
        bs(k, 2, above).start()

    def rows_of(i, who):
        return rows.at[i, row_block(who), :]

    def x_own(i):
        for copy in load(i):
            copy.wait()
        gate = gate_buf[i].astype(jnp.float32)
        act = gate / (1.0 + jnp.exp(-gate))
        rows[i, row_block(x), :] = (act * up_buf[i].astype(jnp.float32)).astype(jnp.bfloat16)
        for way, dx in ((0, 1), (1, -1)):
            remote(rows_of(i, x), rows_of(i, x), x_send.at[i, way], x_recv.at[i, way], at(dx=dx)).start()

    def x_wait(i, way):
        remote(rows_of(i, x), rows_of(i, x), x_send.at[i, way], x_recv.at[i, way], at(dx=1)).wait_recv()

    def x_pass(i):
        way = lax.rem(i + core, 2)
        x_wait(i, way)
        step = 1 - 2 * way
        who = lax.rem(x - step + NX, NX)
        remote(rows_of(i, who), rows_of(i, who), x_send.at[i, 2], x_recv.at[i, 2], at(dx=step)).start()

    def z_hop(j, s, sign):
        long = s < 4
        device = at(dz=sign if long else -sign)
        return remote(z_out.at[j, s], z_in.at[j, s], z_send.at[j, s], z_recv.at[j, s], device)

    def z_block(j, s, sign):
        offset = sign * (4 - s) if s < 4 else -sign * (7 - s)
        return lax.rem(z + offset + NZ, NZ)

    def sign_of(j):
        return 2 * lax.rem(j + core, 2) - 1

    def z_send_block(j, s):
        sign = sign_of(j)
        value = prod[j, z_block(j, s, sign)]
        if s not in (0, 4):
            z_hop(j, s - 1, sign).wait_recv()
            value = value + z_in[j, s - 1].astype(jnp.float32)
        z_out[j, s] = value.astype(jnp.bfloat16)
        z_hop(j, s, sign).start()

    def out_copy(j):
        return pltpu.make_async_copy(total.at[j], out_hbm.at[pl.ds(pl.multiple_of(j * MC, MC), MC), :], out_sem.at[j])

    def z_last(j):
        sign = sign_of(j)
        z_hop(j, 3, sign).wait_recv()
        z_hop(j, 6, sign).wait_recv()
        value = prod[j, z] + z_in[j, 3].astype(jnp.float32) + z_in[j, 6].astype(jnp.float32)
        total[j] = value * (1.0 / (NZ * NX))
        out_copy(j).start()

    def product(j):
        x_wait(j, 1 - lax.rem(j + core, 2))
        x_wait(j, 2)
        turned[...] = rows[j].T
        wide = 2 * NB

        def part(n, carry):
            at_n = pl.ds(pl.multiple_of(n * wide, wide), wide)
            value = jnp.dot(turned[...], cols[:, at_n], preferred_element_type=jnp.float32)
            prod[j, 2 * n] = value[:, :NB]
            prod[j, 2 * n + 1] = value[:, NB:]
            return carry

        lax.fori_loop(0, NZ // 2, part, 0)

    def if_chunk(j, body):
        pl.when((j >= 0) & (j < chunks))(lambda: body(j))

    def z_step(j):
        if_chunk(j - 4 * LAG, z_last)
        for s in (3, 2, 1):
            def middle(i, s=s):
                z_send_block(i, s)
                if s < 3:
                    z_send_block(i, 4 + s)
            if_chunk(j - s * LAG, middle)

        def first(i):
            product(i)
            z_send_block(i, 0)
            z_send_block(i, 4)
        if_chunk(j, first)

    own_copy.wait()
    spread(0)
    x_own(0)
    x_own(1)
    for k in (1, 2):
        bx(k - 1, 1).wait_recv()
        spread(k)
    x_pass(0)
    x_own(2)
    bx(2, 1).wait_recv()
    spread(3)
    spread_on(0)
    x_pass(1)
    x_own(3)
    spread_on(1)
    spread_on(2)
    x_pass(2)
    x_own(4)
    spread_on(3)
    for k in range(NX):
        by(k, 2, across, 1).wait_recv()
        bs(k, 3, across).start()
    x_pass(3)
    for k in range(NX):
        for source in range(4):
            bs(k, source, mine).wait_recv()

    def step(v, carry):
        n = AHEAD + 2 * (v // 3) + v % 3
        take = v % 3 < 2
        pl.when(take & (n <= chunks))(lambda: x_pass(n - 1))
        pl.when(take & (n < chunks))(lambda: x_own(n))
        z_step(v - 2)
        return carry

    lax.fori_loop(0, chunks + 2 + 4 * LAG, step, 0)

    for k in range(3):
        bx(k, 1).wait_send()
    for k in range(NX):
        for which in range(3):
            by(k, which, mine, 1).wait_send()
        for source in range(4):
            bs(k, source, mine).wait_send()

    def drain(i, carry):
        for way in range(3):
            remote(rows_of(i, x), rows_of(i, x), x_send.at[i, way], x_recv.at[i, way], at(dx=1)).wait_send()
        for s in range(7):
            z_hop(i, s, 1).wait_send()
        out_copy(i).wait()
        return carry

    lax.fori_loop(0, chunks, drain, 0)


def solution(mesh):
    def shards(gate_pre, up_pre, out_grad):
        tokens, hidden = gate_pre.shape
        chunks = hidden // MC
        depth = NX * tokens
        dma = pltpu.SemaphoreType.DMA
        hbm = pl.BlockSpec(memory_space=pl.ANY)
        return pl.pallas_call(
            kernel,
            out_shape=jax.ShapeDtypeStruct((hidden, NB), jnp.float32),
            in_specs=[hbm] * 3,
            out_specs=hbm,
            scratch_shapes=[
                pltpu.VMEM((chunks, tokens, MC), jnp.bfloat16),
                pltpu.VMEM((chunks, tokens, MC), jnp.bfloat16),
                pltpu.VMEM((chunks, depth, MC), jnp.bfloat16),
                pltpu.VMEM((MC, depth), jnp.bfloat16),
                pltpu.VMEM((depth, NZ * NB), jnp.bfloat16),
                pltpu.VMEM((chunks, NZ, MC, NB), jnp.float32),
                pltpu.VMEM((chunks, 7, MC, NB), jnp.bfloat16),
                pltpu.VMEM((chunks, 7, MC, NB), jnp.bfloat16),
                pltpu.VMEM((chunks, MC, NB), jnp.float32),
                dma((2, chunks)),
                dma,
                dma((chunks, 3)),
                dma((chunks, 3)),
                dma((3,)),
                dma((3,)),
                dma((NX, 3)),
                dma((NX, 3)),
                dma((NX, 4)),
                dma((NX, 4)),
                dma((chunks, 7)),
                dma((chunks, 7)),
                dma((chunks,)),
            ],
            compiler_params=pltpu.CompilerParams(
                collective_id=0, has_side_effects=True, vmem_limit_bytes=60 * 1024 * 1024
            ),
        )(gate_pre, up_pre, out_grad)

    return jax.shard_map(
        shards,
        mesh=mesh,
        in_specs=(P("node", "local"), P("node", "local"), P("node", "local")),
        out_specs=P("local", "node"),
        check_vma=False,
    )
```

time: 266 us -> 104 us (0.39)
  the two profiles are of different devices: /device:TPU:1 before, /device:TPU:2 now
where the time goes in v1:
time: 104 us
  Pallas kernels  102 us (98%)
  local copies, waits for them, and re-layouts  2.21 us (2%)
    pallas_call x1, Pallas kernels, shards(): pl.pallas_call(kernel, out_shape=jax.ShapeDtypeStruct((hidden, NB), jnp.f...  102 us
    unnamed x1, local copies, waits for them, and re-layouts  2.21 us

profile of v1, /device:TPU:2, one launch (start us, length us, event | category | flops | bytes accessed | tf_op | source)
XLA Modules:
  0.0 104.0 jit_solution(17954018976018038480)
XLA Ops:
  0.0 101.7 %shard_map.37 = f32[1920,128]{1,0:T(8,128)} custom-call(bf16[448,1920]{1,0:T(8,128)(2,1)} %gate_hbm.1, bf16[448,1920]{1,0:T(8,128)(2,1)} %up_hbm.1, bf16[448,512]{1,0:T(8,128)(2,1)} %grad_hbm.1), custom_call_target="tpu_custom_call" | custom-call | tf_op jit(solution)/shard_map/pallas_call | solution.py:253
  101.8 2.2 %copy.5 = f32[1920,128]{1,0:T(8,128)} copy(f32[1920,128]{1,0:T(8,128)} %shard_map.37) | data formatting | bytes 1966080

commit v2 on v0

v2 whole, which is shorter than its diff:
```python
import jax
import jax.numpy as jnp
from jax import lax
from jax.experimental import pallas as pl
from jax.experimental.pallas import tpu as pltpu
from jax.sharding import PartitionSpec as P

MESH = pl.DeviceIdType.MESH
NZ, NX, NY, NC = 8, 4, 4, 2
MC = 128
NB = 128
CHUNKS = 15
PAIRS = 4
ITEMS = CHUNKS - PAIRS
UNITS = [(i, 0) for i in range(PAIRS)] + [(i, 1) for i in range(PAIRS)] + [(i, 0) for i in range(PAIRS, ITEMS)]
QUICK = 0
VMEM_BYTES = 50_000_000
ORDER = (
    ("b_start", 0), ("b_own", 0, 0), ("hide",), ("x_own", 0), ("x_own", 1), ("x_own", 2), ("b_start", 1),
    ("b_own", 0, 1), ("b_pass", 0, 0), ("b_own", 0, 2), ("x_pass", 0), ("b_own", 0, 3), ("b_pass", 0, 1),
    ("x_pass", 1), ("b_far", 0, 0), ("b_pass", 0, 2), ("x_pass", 2), ("b_pass", 0, 3), ("b_own", 1, 0),
    ("b_own", 1, 2), ("b_own", 1, 1), ("b_far", 0, 1), ("b_far", 0, 2), ("x_own", 3), ("b_far", 0, 3),
    ("b_own", 1, 3), ("x_own", 4), ("b_pass", 1, 0), ("b_done", 0), ("product", 0), ("x_pass", 3), ("product", 1),
    ("b_pass", 1, 2), ("x_own", 5), ("product", 2), ("b_pass", 1, 1), ("x_pass", 4), ("mid", 0, 1), ("x_own", 6),
    ("mid", 1, 1), ("b_pass", 1, 3), ("b_far", 1, 0), ("mid", 2, 1), ("x_own", 7), ("product", 3), ("b_far", 1, 2),
    ("x_own", 8), ("mid", 0, 2), ("b_far", 1, 1), ("mid", 1, 2), ("x_pass", 5), ("x_pass", 6), ("mid", 2, 2),
    ("b_far", 1, 3), ("product", 8), ("mid", 0, 3), ("mid", 1, 3), ("mid", 3, 1), ("b_done", 1), ("product", 4),
    ("x_own", 9), ("mid", 2, 3), ("product", 5), ("x_pass", 7), ("x_pass", 8), ("mid", 8, 1), ("product", 6),
    ("mid", 3, 2), ("mid", 4, 1), ("x_own", 10), ("last", 0), ("last", 1), ("last", 2), ("product", 7), ("mid", 5, 1),
    ("mid", 8, 2), ("product", 9), ("mid", 3, 3), ("mid", 6, 1), ("product", 10), ("x_pass", 9), ("mid", 4, 2),
    ("mid", 7, 1), ("mid", 5, 2), ("product", 11), ("x_pass", 10), ("mid", 8, 3), ("mid", 9, 1), ("last", 3),
    ("product", 12), ("mid", 6, 2), ("mid", 10, 1), ("product", 13), ("mid", 4, 3), ("mid", 5, 3), ("mid", 7, 2),
    ("product", 14), ("mid", 11, 1), ("last", 8), ("mid", 9, 2), ("mid", 12, 1), ("mid", 6, 3), ("mid", 10, 2),
    ("mid", 13, 1), ("last", 4), ("last", 5), ("mid", 7, 3), ("mid", 14, 1), ("mid", 11, 2), ("mid", 9, 3),
    ("o_last", 0), ("mid", 12, 2), ("last", 6), ("o_last", 1), ("mid", 10, 3), ("mid", 13, 2), ("last", 7),
    ("mid", 14, 2), ("mid", 11, 3), ("last", 9), ("mid", 12, 3), ("o_last", 2), ("last", 10), ("mid", 13, 3),
    ("mid", 14, 3), ("o_last", 3), ("last", 11), ("last", 12), ("last", 13), ("last", 14),
)


def kernel(
    gate_hbm, up_hbm, grad_hbm, out_ref,
    gate_buf, up_buf, grad_buf, rows, turned, cols, prod, z_out, z_in, o_out, o_in,
    load_sem, grad_sem, x_send, x_recv, b_send, bx_recv, by_recv, bs_recv, z_send, z_recv, o_send, o_recv,
):
    tokens = grad_hbm.shape[0]
    node, local = lax.axis_index("node"), lax.axis_index("local")
    z, x = node // NX, node % NX
    y, core = local // NC, local % NC
    mine = y * NC + core

    def at(dz=0, dx=0, dy=0, dc=0):
        return {
            "node": lax.rem(z + dz + NZ, NZ) * NX + lax.rem(x + dx + NX, NX),
            "local": lax.rem(y + dy + NY, NY) * NC + lax.rem(core + dc, NC),
        }

    def remote(src, dst, send, recv, device):
        return pltpu.make_async_remote_copy(
            src_ref=src, dst_ref=dst, send_sem=send, recv_sem=recv, device_id=device, device_id_type=MESH
        )

    def arrived(ref, sem):
        remote(ref, ref, x_send, sem, at(dx=1)).wait_recv()

    def lanes(block):
        return pl.ds(pl.multiple_of(block * NB, NB), NB)

    def row_block(who):
        return pl.ds(pl.multiple_of(who * tokens, tokens), tokens)

    x_of = (x, lax.rem(x + NX - 1, NX), lax.rem(x + 1, NX), lax.rem(x + 2, NX))

    def piece(n, k, block):
        return cols.at[n, row_block(x_of[k]), lanes(block)]

    below = lax.rem(y + NY - 1, NY) * NC + core
    above = lax.rem(y + 1, NY) * NC + core
    across = lax.rem(y + 2, NY) * NC + core

    def b_start(n):
        for k, dx in ((0, 1), (1, -1), (2, 2)):
            block = lax.rem(x + dx + 2 * n + NX, NX)
            remote(grad_buf.at[block], piece(n, 0, mine), b_send.at[0], bx_recv.at[n, k], at(dx=dx)).start()

    def b_along(n, k, block, sem, dy):
        remote(piece(n, k, block), piece(n, k, block), b_send.at[1], sem, at(dy=dy)).start()

    def b_over(n, k, block):
        remote(piece(n, k, block), piece(n, k, block), b_send.at[2], bs_recv.at[n], at(dc=1)).start()

    def b_own(n, k):
        if k:
            with jax.named_scope(f"bx_{n}{k}"):
                arrived(grad_buf.at[0], bx_recv.at[n, k - 1])
        b_along(n, k, mine, by_recv.at[n, k, 0], 1)
        b_along(n, k, mine, by_recv.at[n, k, 0], -1)
        b_over(n, k, mine)

    def b_pass(n, k):
        with jax.named_scope(f"by_{n}{k}"):
            arrived(rows.at[0, pl.ds(0, 2 * tokens), :], by_recv.at[n, k, 0])
        up = lax.rem(core + k, 2) == 0
        b_along(n, k, jnp.where(up, below, above), by_recv.at[n, k, 1], jnp.where(up, 1, -1))
        b_over(n, k, below)
        b_over(n, k, above)

    def b_far(n, k):
        with jax.named_scope(f"bf_{n}{k}"):
            arrived(grad_buf.at[0], by_recv.at[n, k, 1])
        b_over(n, k, across)

    def b_done(n):
        with jax.named_scope(f"bs_{n}"):
            arrived(rows.at[pl.ds(0, NX)], bs_recv.at[n])

    def rows_of(i, who):
        return rows.at[i, row_block(who), :]

    pair_step = 1 - 2 * lax.rem(x + core, 2)
    half = lax.rem(x - core + NX, NX) // 2

    def chunk_of(n):
        return 2 * n + half if n < PAIRS else n + PAIRS

    def step_of(n):
        return pair_step if n < PAIRS or n % 2 == 0 else -pair_step

    def x_own(n):
        mine_of, other = chunk_of(n), 2 * n + 1 - half if n < PAIRS else chunk_of(n)
        remote(rows_of(other, x), rows_of(other, x), x_send, x_recv.at[n, 0], at(dx=-step_of(n))).start()
        remote(rows_of(mine_of, x), rows_of(mine_of, x), x_send, x_recv.at[n, 1], at(dx=step_of(n))).start()

    def x_pass(n):
        with jax.named_scope("x_pass"):
            arrived(rows_of(0, x), x_recv.at[n, 0])
        block = rows_of(chunk_of(n), lax.rem(x - step_of(n) + NX, NX))
        remote(block, block, x_send, x_recv.at[n, 1], at(dx=step_of(n))).start()

    sign = 2 * core - 1

    def z_move(u, slot, hop, sem):
        remote(z_out.at[u, slot], z_in.at[u, slot], z_send, z_recv.at[u, sem], at(dz=hop * sign)).start()

    def z_wait(u, count, sem):
        with jax.named_scope(f"z_{sem}"):
            arrived(z_in.at[u, pl.ds(0, count)], z_recv.at[u, sem])

    def z_put(u, slot, offset, *added):
        value = prod[u, lax.rem(z + offset * sign + NZ, NZ)]
        for other in added:
            value = value + z_in[u, other].astype(jnp.float32)
        z_out[u, slot] = value.astype(jnp.bfloat16)

    def is_quick(u):
        return u >= CHUNKS - QUICK

    def first(u):
        if is_quick(u):
            moves = ((0, 4, 2, 0), (4, -3, -2, 0), (1, 3, 1, 0), (5, -2, -1, 0), (3, 1, 1, 3))
        else:
            moves = ((0, 4, 1, 0), (4, -3, -1, 0))
        for slot, offset, hop, sem in moves:
            z_put(u, slot, offset)
            z_move(u, slot, hop, sem)

    def mid(u, s):
        z_wait(u, 2 if s < 3 else 1, s - 1)
        z_put(u, s, 4 - s, s - 1)
        z_move(u, s, 1, s if s < 3 else 3)
        if s < 3:
            z_put(u, 4 + s, s - 3, 3 + s)
            z_move(u, 4 + s, -1, s if s < 2 else 3)

    def qmid(u):
        z_wait(u, 4, 0)
        z_put(u, 2, 2, 0, 1)
        z_move(u, 2, 2, 3)
        z_put(u, 6, -1, 4, 5)
        z_move(u, 6, -1, 3)

    def out_rows(chunk):
        return pl.ds(pl.multiple_of(chunk * MC, MC), MC)

    def last(u):
        added = (2, 3, 6) if is_quick(u) else (3, 6)
        z_wait(u, len(added), 3)
        value = prod[u, z]
        for other in added:
            value = value + z_in[u, other].astype(jnp.float32)
        value = value * (1.0 / (NZ * NX))
        n, second = UNITS[u]
        if second:
            o_out[n] = value.astype(jnp.bfloat16)
            remote(o_out.at[n], o_in.at[n], o_send, o_recv.at[n], at(dx=2)).start()
        else:
            out_ref[out_rows(chunk_of(n)), :] = value

    def o_last(n):
        with jax.named_scope("o"):
            arrived(o_in.at[0], o_recv.at[n])
        out_ref[out_rows(2 * n + 1 - half), :] = o_in[n].astype(jnp.float32)

    def product(u):
        n, second = UNITS[u]
        if not second:
            with jax.named_scope("x_last"):
                arrived(rows.at[0, pl.ds(0, 2 * tokens), :], x_recv.at[n, 1])
        turned[...] = rows[chunk_of(n)].T
        wide = 2 * NB

        def part(i, carry):
            at_i = pl.ds(pl.multiple_of(i * wide, wide), wide)
            value = jnp.dot(turned[...], cols[second, :, at_i], preferred_element_type=jnp.float32)
            prod[u, 2 * i] = value[:, :NB]
            prod[u, 2 * i + 1] = value[:, NB:]
            return carry

        with jax.named_scope("dot"):
            lax.fori_loop(0, NZ // 2, part, 0)
        first(u)

    def load(i):
        return (
            pltpu.make_async_copy(gate_hbm.at[:, lanes(i)], gate_buf.at[i], load_sem.at[i]),
            pltpu.make_async_copy(up_hbm.at[:, lanes(i)], up_buf.at[i], load_sem.at[i]),
        )

    def hide():
        def one(i, carry):
            for copy in load(i):
                copy.wait()
            gate = gate_buf[i].astype(jnp.float32)
            act = gate / (1.0 + jnp.exp(-gate))
            rows[i, row_block(x), :] = (act * up_buf[i].astype(jnp.float32)).astype(jnp.bfloat16)
            return carry

        for i in range(CHUNKS):
            for copy in load(i):
                copy.start()
        if PAIRS:
            cols[1, row_block(x), lanes(mine)] = grad_buf[lax.rem(x + 2, NX)]
        with jax.named_scope("hide"):
            lax.fori_loop(0, CHUNKS, one, 0)

    partners = (
        at(dz=1), at(dz=-1), at(dz=2), at(dz=-2), at(dx=1), at(dx=-1), at(dx=2), at(dy=1), at(dy=-1), at(dc=1),
    )
    barrier = pltpu.get_barrier_semaphore()
    for device in partners:
        pl.semaphore_signal(barrier, inc=1, device_id=device, device_id_type=MESH)
    grad_copy = [
        pltpu.make_async_copy(grad_hbm.at[:, pl.ds(k * NB, NB)], grad_buf.at[k], grad_sem) for k in range(NX)
    ]
    for copy in grad_copy:
        copy.start()
    with jax.named_scope("grad"):
        pltpu.make_async_copy(grad_buf, grad_buf, grad_sem).wait()
    cols[0, row_block(x), lanes(mine)] = grad_buf[x]
    with jax.named_scope("barrier"):
        pl.semaphore_wait(barrier, len(partners))

    steps = {
        "b_start": b_start, "b_own": b_own, "b_pass": b_pass, "b_far": b_far, "b_done": b_done, "hide": hide,
        "x_own": x_own, "x_pass": x_pass, "product": product, "mid": mid, "qmid": qmid, "last": last, "o_last": o_last,
    }
    for name, *arguments in ORDER:
        steps[name](*arguments)

    def sent(ref, sem):
        remote(ref, ref, sem, x_recv.at[0, 0], at(dx=1)).wait_send()

    with jax.named_scope("sent"):
        sent(rows.at[pl.ds(0, ITEMS), pl.ds(0, 3 * tokens), :], x_send)
        sets = 2 if PAIRS else 1
        sent(rows.at[pl.ds(0, sets), pl.ds(0, 3 * tokens), :], b_send.at[0])
        sent(rows.at[pl.ds(0, 3 * sets)], b_send.at[1])
        sent(rows.at[pl.ds(0, 4 * sets)], b_send.at[2])
        sent(z_out, z_send)
        if PAIRS:
            sent(o_out, o_send)


def solution(mesh):
    def shards(gate_pre, up_pre, out_grad):
        tokens, hidden = gate_pre.shape
        depth = NX * tokens
        dma = pltpu.SemaphoreType.DMA
        operands = [pltpu.with_memory_space_constraint(a, pltpu.HBM) for a in (gate_pre, up_pre, out_grad)]
        return pl.pallas_call(
            kernel,
            out_shape=jax.ShapeDtypeStruct((hidden, NB), jnp.float32),
            in_specs=[pl.BlockSpec(memory_space=pl.ANY)] * 3,
            out_specs=pl.BlockSpec(memory_space=pltpu.VMEM),
            scratch_shapes=[
                pltpu.VMEM((CHUNKS, tokens, MC), jnp.bfloat16),
                pltpu.VMEM((CHUNKS, tokens, MC), jnp.bfloat16),
                pltpu.VMEM((NX, tokens, NB), jnp.bfloat16),
                pltpu.VMEM((CHUNKS, depth, MC), jnp.bfloat16),
                pltpu.VMEM((MC, depth), jnp.bfloat16),
                pltpu.VMEM((2, depth, NZ * NB), jnp.bfloat16),
                pltpu.VMEM((CHUNKS, NZ, MC, NB), jnp.float32),
                pltpu.VMEM((CHUNKS, 7, MC, NB), jnp.bfloat16),
                pltpu.VMEM((CHUNKS, 7, MC, NB), jnp.bfloat16),
                pltpu.VMEM((max(PAIRS, 1), MC, NB), jnp.bfloat16),
                pltpu.VMEM((max(PAIRS, 1), MC, NB), jnp.bfloat16),
                dma((CHUNKS,)),
                dma,
                dma,
                dma((ITEMS, 2)),
                dma((3,)),
                dma((2, 3)),
                dma((2, NX, 2)),
                dma((2,)),
                dma,
                dma((CHUNKS, 4)),
                dma,
                dma((max(PAIRS, 1),)),
            ],
            compiler_params=pltpu.CompilerParams(
                collective_id=0, has_side_effects=True, vmem_limit_bytes=VMEM_BYTES
            ),
        )(*operands)

    return jax.shard_map(
        shards,
        mesh=mesh,
        in_specs=(P("node", "local"), P("node", "local"), P("node", "local")),
        out_specs=P("local", "node"),
        check_vma=False,
    )
```

time: 266 us -> 82.9 us (0.31)
  waiting for transfers between devices: 195 us -> 0 us
  Pallas kernels: 0 us -> 80.8 us
  blocking collectives: 35.6 us -> 0 us
  between operations: 13.5 us -> 0.01 us
  matrix products: 11.6 us -> 0 us
  local copies, waits for them, and re-layouts: 8.99 us -> 0.95 us
    reduce_scatter x1 -> x0, waiting for transfers between devices: 165 us -> none  [sum_by_axis(): running = lax.psum_scatter(running, axis, scatter_dimension=0, tiled=True)]
    pallas_call x0 -> x1, Pallas kernels: none -> 80.8 us  [shards(): pl.pallas_call(kernel, out_shape=jax.ShapeDtypeStruct((hidden, NB), jnp.f...]
    all_to_all x2 -> x0, blocking collectives: 35.6 us -> none  [copy_for_each(): return lax.all_to_all(copies, axis, split_axis=0, concat_axis=0, tiled=True)]
    unnamed x3 -> x0, waiting for transfers between devices: 30 us -> none
    dot_general x1 -> x0, matrix products: 11.6 us -> none  [shards(): lax.dot_general(gathered, hidden, (((0,), (0,)), ((), ())), preferred_ele...]
    unnamed x6 -> x1, local copies, waits for them, and re-layouts: 6.77 us -> 0.95 us
  transfers between devices with their start and end apart: 2 -> 0, of which waited for: 2 -> 0; matrix products, arithmetic and copies ran while one was open for 0% -> 0% of each run, Pallas kernels for 0% -> 0%
where the time goes in v2:
time: 82.9 us; the launch traced here: 81.8 us
  Pallas kernels  80.8 us (97%)
  local copies, waits for them, and re-layouts  0.95 us (1%)
    pallas_call x1, Pallas kernels, shards(): pl.pallas_call(kernel, out_shape=jax.ShapeDtypeStruct((hidden, NB), jnp.f...  80.8 us

profile of v2, /device:TPU:1, one launch (start us, length us, event | category | flops | bytes accessed | tf_op | source)
XLA Modules:
  0.0 81.8 jit_solution(11189357337723984850)
XLA Ops:
  0.0 80.8 %shard_map.37 = f32[1920,128]{1,0:T(8,128)S(1)} custom-call(bf16[448,1920]{1,0:T(8,128)(2,1)} %gate_hbm.1, bf16[448,1920]{1,0:T(8,128)(2,1)} %up_hbm.1, bf16[448,512]{1,0:T(8,128)(2,1)} %grad_hbm.1), custom_call_target="tpu_custom_call" | custom-call | tf_op jit(solution)/shard_map/pallas_call | solution.py:290
  80.9 0.9 %copy.5 = f32[1920,128]{1,0:T(8,128)} copy(f32[1920,128]{1,0:T(8,128)S(1)} %shard_map.37) | data formatting | bytes 1966080

commit v3 on v2

--- a/solution.py
+++ b/solution.py
@@ -10,31 +10,37 @@
 MC = 128
 NB = 128
 CHUNKS = 15
-PAIRS = 4
+PAIRS = 7
 ITEMS = CHUNKS - PAIRS
 UNITS = [(i, 0) for i in range(PAIRS)] + [(i, 1) for i in range(PAIRS)] + [(i, 0) for i in range(PAIRS, ITEMS)]
+SPLIT = (0, 1, 7, 8)
 QUICK = 0
 VMEM_BYTES = 50_000_000
 ORDER = (
-    ("b_start", 0), ("b_own", 0, 0), ("hide",), ("x_own", 0), ("x_own", 1), ("x_own", 2), ("b_start", 1),
-    ("b_own", 0, 1), ("b_pass", 0, 0), ("b_own", 0, 2), ("x_pass", 0), ("b_own", 0, 3), ("b_pass", 0, 1),
-    ("x_pass", 1), ("b_far", 0, 0), ("b_pass", 0, 2), ("x_pass", 2), ("b_pass", 0, 3), ("b_own", 1, 0),
-    ("b_own", 1, 2), ("b_own", 1, 1), ("b_far", 0, 1), ("b_far", 0, 2), ("x_own", 3), ("b_far", 0, 3),
-    ("b_own", 1, 3), ("x_own", 4), ("b_pass", 1, 0), ("b_done", 0), ("product", 0), ("x_pass", 3), ("product", 1),
-    ("b_pass", 1, 2), ("x_own", 5), ("product", 2), ("b_pass", 1, 1), ("x_pass", 4), ("mid", 0, 1), ("x_own", 6),
-    ("mid", 1, 1), ("b_pass", 1, 3), ("b_far", 1, 0), ("mid", 2, 1), ("x_own", 7), ("product", 3), ("b_far", 1, 2),
-    ("x_own", 8), ("mid", 0, 2), ("b_far", 1, 1), ("mid", 1, 2), ("x_pass", 5), ("x_pass", 6), ("mid", 2, 2),
-    ("b_far", 1, 3), ("product", 8), ("mid", 0, 3), ("mid", 1, 3), ("mid", 3, 1), ("b_done", 1), ("product", 4),
-    ("x_own", 9), ("mid", 2, 3), ("product", 5), ("x_pass", 7), ("x_pass", 8), ("mid", 8, 1), ("product", 6),
-    ("mid", 3, 2), ("mid", 4, 1), ("x_own", 10), ("last", 0), ("last", 1), ("last", 2), ("product", 7), ("mid", 5, 1),
-    ("mid", 8, 2), ("product", 9), ("mid", 3, 3), ("mid", 6, 1), ("product", 10), ("x_pass", 9), ("mid", 4, 2),
-    ("mid", 7, 1), ("mid", 5, 2), ("product", 11), ("x_pass", 10), ("mid", 8, 3), ("mid", 9, 1), ("last", 3),
-    ("product", 12), ("mid", 6, 2), ("mid", 10, 1), ("product", 13), ("mid", 4, 3), ("mid", 5, 3), ("mid", 7, 2),
-    ("product", 14), ("mid", 11, 1), ("last", 8), ("mid", 9, 2), ("mid", 12, 1), ("mid", 6, 3), ("mid", 10, 2),
-    ("mid", 13, 1), ("last", 4), ("last", 5), ("mid", 7, 3), ("mid", 14, 1), ("mid", 11, 2), ("mid", 9, 3),
-    ("o_last", 0), ("mid", 12, 2), ("last", 6), ("o_last", 1), ("mid", 10, 3), ("mid", 13, 2), ("last", 7),
-    ("mid", 14, 2), ("mid", 11, 3), ("last", 9), ("mid", 12, 3), ("o_last", 2), ("last", 10), ("mid", 13, 3),
-    ("mid", 14, 3), ("o_last", 3), ("last", 11), ("last", 12), ("last", 13), ("last", 14),
+    ("b_near", 0), ("b_own", 0, 0), ("hide",), ("b_far2", 0), ("b_own", 1, 0), ("b_near", 1), ("b_own", 0, 2),
+    ("b_far2", 1), ("b_own", 0, 1), ("x_own", 0), ("x_own", 1), ("x_own", 2), ("b_own", 0, 3), ("b_own", 1, 1),
+    ("b_own", 1, 2), ("x_pass", 0), ("b_own", 1, 3), ("b_take", 0, 1), ("b_pass", 0, 1), ("x_pass", 1),
+    ("b_take", 0, 3), ("x_own", 3), ("b_take", 1, 1), ("b_take", 0, 0), ("b_pass", 0, 0), ("b_take", 0, 2),
+    ("b_most", 0), ("b_take", 1, 0), ("x_pass", 2), ("b_pass", 0, 2), ("x_own", 4), ("b_pass", 0, 3),
+    ("b_pass", 1, 1), ("part", 0, 0), ("b_pass", 1, 0), ("b_take", 1, 2), ("b_pass", 1, 2), ("x_pass", 3),
+    ("b_take", 1, 3), ("b_pass", 1, 3), ("part", 1, 0), ("b_most", 1), ("part", 7, 0), ("b_far", 0, 1), ("x_pass", 4),
+    ("b_far", 0, 2), ("x_own", 5), ("b_far", 0, 3), ("x_own", 6), ("b_far", 0, 0), ("part", 8, 0), ("pmid", 0, 1, 0),
+    ("b_rest", 0), ("product", 2), ("b_far", 1, 0), ("part", 1, 1), ("pmid", 7, 1, 0), ("product", 3),
+    ("b_far", 1, 1), ("pmid", 1, 1, 0), ("part", 0, 1), ("b_far", 1, 2), ("b_far", 1, 3), ("x_pass", 5),
+    ("pmid", 8, 1, 0), ("product", 4), ("x_own", 7), ("mid", 2, 1), ("b_rest", 1), ("part", 8, 1), ("pmid", 7, 2, 0),
+    ("product", 9), ("x_pass", 6), ("mid", 3, 1), ("product", 10), ("product", 11), ("mid", 4, 1), ("product", 5),
+    ("product", 12), ("part", 7, 1), ("pmid", 0, 1, 1), ("mid", 9, 1), ("pmid", 8, 2, 0), ("mid", 10, 1),
+    ("product", 6), ("x_pass", 7), ("product", 13), ("mid", 11, 1), ("mid", 12, 1), ("pmid", 7, 1, 1), ("mid", 5, 1),
+    ("mid", 10, 2), ("mid", 2, 2), ("pmid", 8, 1, 1), ("pmid", 1, 2, 0), ("mid", 13, 1), ("product", 14),
+    ("mid", 11, 2), ("pmid", 7, 2, 1), ("mid", 12, 2), ("mid", 9, 2), ("mid", 3, 2), ("mid", 10, 3),
+    ("pmid", 8, 2, 1), ("mid", 13, 2), ("pmid", 1, 1, 1), ("pmid", 7, 3, 0), ("pmid", 0, 2, 1), ("mid", 14, 1),
+    ("mid", 11, 3), ("mid", 6, 1), ("pmid", 8, 3, 0), ("mid", 12, 3), ("pmid", 7, 3, 1), ("mid", 9, 3),
+    ("mid", 13, 3), ("mid", 4, 2), ("pmid", 8, 3, 1), ("last", 10), ("mid", 5, 2), ("mid", 14, 2), ("mid", 6, 2),
+    ("pmid", 1, 2, 1), ("last", 11), ("pmid", 0, 2, 0), ("last", 12), ("plast", 7), ("mid", 2, 3), ("mid", 3, 3),
+    ("last", 13), ("pmid", 1, 3, 0), ("last", 9), ("mid", 4, 3), ("pmid", 0, 3, 1), ("plast", 8), ("mid", 5, 3),
+    ("mid", 14, 3), ("mid", 6, 3), ("pmid", 1, 3, 1), ("o_last", 3), ("pmid", 0, 3, 0), ("last", 2), ("o_last", 4),
+    ("o_last", 5), ("o_last", 0), ("last", 5), ("last", 3), ("o_last", 6), ("last", 4), ("o_last", 1), ("o_last", 2),
+    ("last", 14), ("plast", 1), ("last", 6), ("plast", 0),
 )
 
 
@@ -78,16 +84,22 @@
     above = lax.rem(y + 1, NY) * NC + core
     across = lax.rem(y + 2, NY) * NC + core
 
-    def b_start(n):
-        for k, dx in ((0, 1), (1, -1), (2, 2)):
-            block = lax.rem(x + dx + 2 * n + NX, NX)
-            remote(grad_buf.at[block], piece(n, 0, mine), b_send.at[0], bx_recv.at[n, k], at(dx=dx)).start()
+    def b_send_to(n, k, dx):
+        block = lax.rem(x + dx + 2 * n + NX, NX)
+        remote(grad_buf.at[block], piece(n, 0, mine), b_send.at[0], bx_recv.at[n, k], at(dx=dx)).start()
+
+    def b_near(n):
+        b_send_to(n, 0, 1)
+        b_send_to(n, 1, -1)
+
+    def b_far2(n):
+        b_send_to(n, 2, 2)
 
     def b_along(n, k, block, sem, dy):
         remote(piece(n, k, block), piece(n, k, block), b_send.at[1], sem, at(dy=dy)).start()
 
-    def b_over(n, k, block):
-        remote(piece(n, k, block), piece(n, k, block), b_send.at[2], bs_recv.at[n], at(dc=1)).start()
+    def b_over(n, k, block, part=0):
+        remote(piece(n, k, block), piece(n, k, block), b_send.at[2], bs_recv.at[n, part], at(dc=1)).start()
 
     def b_own(n, k):
         if k:
@@ -97,22 +109,28 @@
         b_along(n, k, mine, by_recv.at[n, k, 0], -1)
         b_over(n, k, mine)
 
-    def b_pass(n, k):
+    def b_take(n, k):
         with jax.named_scope(f"by_{n}{k}"):
             arrived(rows.at[0, pl.ds(0, 2 * tokens), :], by_recv.at[n, k, 0])
+        b_over(n, k, below)
+        b_over(n, k, above)
+
+    def b_pass(n, k):
         up = lax.rem(core + k, 2) == 0
         b_along(n, k, jnp.where(up, below, above), by_recv.at[n, k, 1], jnp.where(up, 1, -1))
-        b_over(n, k, below)
-        b_over(n, k, above)
 
     def b_far(n, k):
         with jax.named_scope(f"bf_{n}{k}"):
             arrived(grad_buf.at[0], by_recv.at[n, k, 1])
-        b_over(n, k, across)
-
-    def b_done(n):
-        with jax.named_scope(f"bs_{n}"):
-            arrived(rows.at[pl.ds(0, NX)], bs_recv.at[n])
+        b_over(n, k, across, 1)
+
+    def b_most(n):
+        with jax.named_scope(f"bm_{n}"):
+            arrived(rows.at[pl.ds(0, 3)], bs_recv.at[n, 0])
+
+    def b_rest(n):
+        with jax.named_scope(f"br_{n}"):
+            arrived(rows.at[0], bs_recv.at[n, 1])
 
     def rows_of(i, who):
         return rows.at[i, row_block(who), :]
@@ -139,15 +157,21 @@
 
     sign = 2 * core - 1
 
+    def z_sem(u, sem):
+        return z_recv.at[4 * u + 2 * sum(v < u for v in SPLIT) + sem]
+
     def z_move(u, slot, hop, sem):
-        remote(z_out.at[u, slot], z_in.at[u, slot], z_send, z_recv.at[u, sem], at(dz=hop * sign)).start()
+        remote(z_out.at[u, slot], z_in.at[u, slot], z_send, z_sem(u, sem), at(dz=hop * sign)).start()
 
     def z_wait(u, count, sem):
         with jax.named_scope(f"z_{sem}"):
-            arrived(z_in.at[u, pl.ds(0, count)], z_recv.at[u, sem])
+            arrived(z_in.at[u, pl.ds(0, count)], z_sem(u, sem))
+
+    def block_at(offset):
+        return lax.rem(z + offset * sign + NZ, NZ)
 
     def z_put(u, slot, offset, *added):
-        value = prod[u, lax.rem(z + offset * sign + NZ, NZ)]
+        value = prod[u, block_at(offset)]
         for other in added:
             value = value + z_in[u, other].astype(jnp.float32)
         z_out[u, slot] = value.astype(jnp.bfloat16)
@@ -178,6 +202,32 @@
         z_move(u, 2, 2, 3)
         z_put(u, 6, -1, 4, 5)
         z_move(u, 6, -1, 3)
+
+    def if_part(offset, part, body):
+        far = block_at(offset) // NC == lax.rem(y + 2, NY)
+        pl.when(far if part else jnp.logical_not(far))(body)
+
+    def pfirst(u, part):
+        for slot, offset, hop, sem in ((0, 4, 1, 0), (4, -3, -1, 4)):
+            def body(slot=slot, offset=offset, hop=hop, sem=sem):
+                z_put(u, slot, offset)
+                z_move(u, slot, hop, sem)
+            if_part(offset, part, body)
+
+    def pmid(u, s, part):
+        def long():
+            z_wait(u, 1, s - 1)
+            z_put(u, s, 4 - s, s - 1)
+            z_move(u, s, 1, s)
+
+        def short():
+            z_wait(u, 1, 3 + s)
+            z_put(u, 4 + s, s - 3, 3 + s)
+            z_move(u, 4 + s, -1, 4 + s if s < 2 else 3)
+
+        if_part(4 - s, part, long)
+        if s < 3:
+            if_part(s - 3, part, short)
 
     def out_rows(chunk):
         return pl.ds(pl.multiple_of(chunk * MC, MC), MC)
@@ -201,24 +251,36 @@
             arrived(o_in.at[0], o_recv.at[n])
         out_ref[out_rows(2 * n + 1 - half), :] = o_in[n].astype(jnp.float32)
 
-    def product(u):
+    def rows_ready(u):
         n, second = UNITS[u]
         if not second:
             with jax.named_scope("x_last"):
                 arrived(rows.at[0, pl.ds(0, 2 * tokens), :], x_recv.at[n, 1])
-        turned[...] = rows[chunk_of(n)].T
-        wide = 2 * NB
-
-        def part(i, carry):
-            at_i = pl.ds(pl.multiple_of(i * wide, wide), wide)
-            value = jnp.dot(turned[...], cols[second, :, at_i], preferred_element_type=jnp.float32)
-            prod[u, 2 * i] = value[:, :NB]
-            prod[u, 2 * i + 1] = value[:, NB:]
-            return carry
-
+            turned[min(n, PAIRS)] = rows[chunk_of(n)].T
+
+    def dot(u, place):
+        n, second = UNITS[u]
+        at_place = pl.ds(pl.multiple_of(place * NC * NB, NC * NB), NC * NB)
+        value = jnp.dot(turned[min(n, PAIRS)], cols[second, :, at_place], preferred_element_type=jnp.float32)
+        for i in range(NC):
+            prod[u, NC * place + i] = value[:, i * NB : (i + 1) * NB]
+
+    def product(u):
+        rows_ready(u)
         with jax.named_scope("dot"):
-            lax.fori_loop(0, NZ // 2, part, 0)
+            for place in range(NY):
+                dot(u, place)
         first(u)
+
+    def part(u, part):
+        if part:
+            dot(u, lax.rem(y + 2, NY))
+        else:
+            rows_ready(u)
+            with jax.named_scope("dot"):
+                for step in (0, 1, 3):
+                    dot(u, lax.rem(y + step, NY))
+        pfirst(u, part)
 
     def load(i):
         return (
@@ -261,8 +323,10 @@
         pl.semaphore_wait(barrier, len(partners))
 
     steps = {
-        "b_start": b_start, "b_own": b_own, "b_pass": b_pass, "b_far": b_far, "b_done": b_done, "hide": hide,
-        "x_own": x_own, "x_pass": x_pass, "product": product, "mid": mid, "qmid": qmid, "last": last, "o_last": o_last,
+        "b_near": b_near, "b_far2": b_far2, "b_own": b_own, "b_take": b_take, "b_pass": b_pass, "b_far": b_far,
+        "b_most": b_most, "b_rest": b_rest, "part": part, "pmid": pmid, "plast": last,
+        "hide": hide, "x_own": x_own, "x_pass": x_pass, "product": product, "mid": mid, "qmid": qmid, "last": last,
+        "o_last": o_last,
     }
     for name, *arguments in ORDER:
         steps[name](*arguments)
@@ -297,7 +361,7 @@
                 pltpu.VMEM((CHUNKS, tokens, MC), jnp.bfloat16),
                 pltpu.VMEM((NX, tokens, NB), jnp.bfloat16),
                 pltpu.VMEM((CHUNKS, depth, MC), jnp.bfloat16),
-                pltpu.VMEM((MC, depth), jnp.bfloat16),
+                pltpu.VMEM((PAIRS + 1, MC, depth), jnp.bfloat16),
                 pltpu.VMEM((2, depth, NZ * NB), jnp.bfloat16),
                 pltpu.VMEM((CHUNKS, NZ, MC, NB), jnp.float32),
                 pltpu.VMEM((CHUNKS, 7, MC, NB), jnp.bfloat16),
@@ -311,9 +375,9 @@
                 dma((3,)),
                 dma((2, 3)),
                 dma((2, NX, 2)),
-                dma((2,)),
+                dma((2, 2)),
                 dma,
-                dma((CHUNKS, 4)),
+                dma((4 * CHUNKS + 2 * len(SPLIT),)),
                 dma,
                 dma((max(PAIRS, 1),)),
             ],

time: 82.9 us -> 77.8 us (0.938)
  Pallas kernels: 80.8 us -> 76.1 us
    pallas_call x1, Pallas kernels: 80.8 us -> 76.1 us  [shards(): pl.pallas_call(kernel, out_shape=jax.ShapeDtypeStruct((hidden, NB), jnp.f...]
where the time goes in v3:
time: 77.8 us; the launch traced here: 77.1 us
  Pallas kernels  76.1 us (98%)
  local copies, waits for them, and re-layouts  0.95 us (1%)
    pallas_call x1, Pallas kernels, shards(): pl.pallas_call(kernel, out_shape=jax.ShapeDtypeStruct((hidden, NB), jnp.f...  76.1 us

profile of v3, /device:TPU:1, one launch (start us, length us, event | category | flops | bytes accessed | tf_op | source)
XLA Modules:
  0.0 77.1 jit_solution(11928772569204594586)
XLA Ops:
  0.0 76.1 %shard_map.37 = f32[1920,128]{1,0:T(8,128)S(1)} custom-call(bf16[448,1920]{1,0:T(8,128)(2,1)} %gate_hbm.1, bf16[448,1920]{1,0:T(8,128)(2,1)} %up_hbm.1, bf16[448,512]{1,0:T(8,128)(2,1)} %grad_hbm.1), custom_call_target="tpu_custom_call" | custom-call | tf_op jit(solution)/shard_map/pallas_call | solution.py:354
  76.2 0.9 %copy.5 = f32[1920,128]{1,0:T(8,128)} copy(f32[1920,128]{1,0:T(8,128)S(1)} %shard_map.37) | data formatting | bytes 1966080

commit v4 on v3

--- a/solution.py
+++ b/solution.py
@@ -8,39 +8,39 @@
 MESH = pl.DeviceIdType.MESH
 NZ, NX, NY, NC = 8, 4, 4, 2
 MC = 128
+LOADS = 5
 NB = 128
 CHUNKS = 15
-PAIRS = 7
+PAIRS = 6
 ITEMS = CHUNKS - PAIRS
 UNITS = [(i, 0) for i in range(PAIRS)] + [(i, 1) for i in range(PAIRS)] + [(i, 0) for i in range(PAIRS, ITEMS)]
-SPLIT = (0, 1, 7, 8)
+SPLIT = (0, 1, 6)
 QUICK = 0
 VMEM_BYTES = 50_000_000
 ORDER = (
-    ("b_near", 0), ("b_own", 0, 0), ("hide",), ("b_far2", 0), ("b_own", 1, 0), ("b_near", 1), ("b_own", 0, 2),
-    ("b_far2", 1), ("b_own", 0, 1), ("x_own", 0), ("x_own", 1), ("x_own", 2), ("b_own", 0, 3), ("b_own", 1, 1),
-    ("b_own", 1, 2), ("x_pass", 0), ("b_own", 1, 3), ("b_take", 0, 1), ("b_pass", 0, 1), ("x_pass", 1),
-    ("b_take", 0, 3), ("x_own", 3), ("b_take", 1, 1), ("b_take", 0, 0), ("b_pass", 0, 0), ("b_take", 0, 2),
-    ("b_most", 0), ("b_take", 1, 0), ("x_pass", 2), ("b_pass", 0, 2), ("x_own", 4), ("b_pass", 0, 3),
-    ("b_pass", 1, 1), ("part", 0, 0), ("b_pass", 1, 0), ("b_take", 1, 2), ("b_pass", 1, 2), ("x_pass", 3),
-    ("b_take", 1, 3), ("b_pass", 1, 3), ("part", 1, 0), ("b_most", 1), ("part", 7, 0), ("b_far", 0, 1), ("x_pass", 4),
-    ("b_far", 0, 2), ("x_own", 5), ("b_far", 0, 3), ("x_own", 6), ("b_far", 0, 0), ("part", 8, 0), ("pmid", 0, 1, 0),
-    ("b_rest", 0), ("product", 2), ("b_far", 1, 0), ("part", 1, 1), ("pmid", 7, 1, 0), ("product", 3),
-    ("b_far", 1, 1), ("pmid", 1, 1, 0), ("part", 0, 1), ("b_far", 1, 2), ("b_far", 1, 3), ("x_pass", 5),
-    ("pmid", 8, 1, 0), ("product", 4), ("x_own", 7), ("mid", 2, 1), ("b_rest", 1), ("part", 8, 1), ("pmid", 7, 2, 0),
-    ("product", 9), ("x_pass", 6), ("mid", 3, 1), ("product", 10), ("product", 11), ("mid", 4, 1), ("product", 5),
-    ("product", 12), ("part", 7, 1), ("pmid", 0, 1, 1), ("mid", 9, 1), ("pmid", 8, 2, 0), ("mid", 10, 1),
-    ("product", 6), ("x_pass", 7), ("product", 13), ("mid", 11, 1), ("mid", 12, 1), ("pmid", 7, 1, 1), ("mid", 5, 1),
-    ("mid", 10, 2), ("mid", 2, 2), ("pmid", 8, 1, 1), ("pmid", 1, 2, 0), ("mid", 13, 1), ("product", 14),
-    ("mid", 11, 2), ("pmid", 7, 2, 1), ("mid", 12, 2), ("mid", 9, 2), ("mid", 3, 2), ("mid", 10, 3),
-    ("pmid", 8, 2, 1), ("mid", 13, 2), ("pmid", 1, 1, 1), ("pmid", 7, 3, 0), ("pmid", 0, 2, 1), ("mid", 14, 1),
-    ("mid", 11, 3), ("mid", 6, 1), ("pmid", 8, 3, 0), ("mid", 12, 3), ("pmid", 7, 3, 1), ("mid", 9, 3),
-    ("mid", 13, 3), ("mid", 4, 2), ("pmid", 8, 3, 1), ("last", 10), ("mid", 5, 2), ("mid", 14, 2), ("mid", 6, 2),
-    ("pmid", 1, 2, 1), ("last", 11), ("pmid", 0, 2, 0), ("last", 12), ("plast", 7), ("mid", 2, 3), ("mid", 3, 3),
-    ("last", 13), ("pmid", 1, 3, 0), ("last", 9), ("mid", 4, 3), ("pmid", 0, 3, 1), ("plast", 8), ("mid", 5, 3),
-    ("mid", 14, 3), ("mid", 6, 3), ("pmid", 1, 3, 1), ("o_last", 3), ("pmid", 0, 3, 0), ("last", 2), ("o_last", 4),
-    ("o_last", 5), ("o_last", 0), ("last", 5), ("last", 3), ("o_last", 6), ("last", 4), ("o_last", 1), ("o_last", 2),
-    ("last", 14), ("plast", 1), ("last", 6), ("plast", 0),
+    ("b_near", 0), ("b_own", 0, 0), ("hide",), ("b_own", 1, 0), ("b_far2", 0), ("x_own", 0), ("x_own", 1),
+    ("b_own", 0, 1), ("b_own", 0, 2), ("b_near", 1), ("b_take", 1, 0), ("x_pass", 0), ("b_far2", 1), ("b_own", 0, 3),
+    ("b_take", 0, 1), ("x_pass", 1), ("b_pass", 0, 1), ("b_take", 0, 2), ("b_pass", 0, 2), ("x_own", 2),
+    ("b_own", 1, 2), ("b_take", 0, 3), ("b_take", 0, 0), ("b_most", 0), ("b_own", 1, 1), ("b_pass", 0, 3),
+    ("b_pass", 0, 0), ("x_own", 3), ("part", 0, 0), ("b_far", 0, 1), ("b_far", 0, 2), ("b_take", 1, 2), ("x_pass", 2),
+    ("x_own", 4), ("b_own", 1, 3), ("part", 1, 0), ("b_take", 1, 1), ("pmid", 0, 1, 0), ("b_pass", 1, 2),
+    ("b_far", 0, 0), ("b_pass", 1, 1), ("b_far", 0, 3), ("b_pass", 1, 0), ("x_pass", 3), ("x_pass", 4), ("b_rest", 0),
+    ("part", 1, 1), ("part", 0, 1), ("pmid", 1, 1, 0), ("b_take", 1, 3), ("b_pass", 1, 3), ("x_own", 5),
+    ("pmid", 0, 2, 0), ("product", 2), ("b_most", 1), ("part", 6, 0), ("x_own", 6), ("product", 3), ("pmid", 1, 1, 1),
+    ("b_far", 1, 2), ("pmid", 0, 1, 1), ("pmid", 1, 2, 0), ("b_far", 1, 1), ("b_far", 1, 0), ("product", 4),
+    ("b_far", 1, 3), ("pmid", 0, 3, 0), ("mid", 2, 1), ("x_pass", 5), ("x_own", 7), ("x_own", 8), ("pmid", 6, 1, 0),
+    ("b_rest", 1), ("product", 8), ("x_pass", 6), ("mid", 3, 1), ("product", 7), ("part", 6, 1), ("mid", 4, 1),
+    ("product", 10), ("pmid", 1, 2, 1), ("product", 9), ("mid", 8, 1), ("product", 5), ("x_pass", 7), ("x_pass", 8),
+    ("pmid", 6, 1, 1), ("mid", 2, 2), ("product", 11), ("mid", 10, 1), ("pmid", 0, 2, 1), ("pmid", 6, 2, 0),
+    ("mid", 9, 1), ("mid", 7, 1), ("mid", 5, 1), ("product", 12), ("mid", 11, 1), ("mid", 8, 2), ("product", 14),
+    ("product", 13), ("pmid", 6, 2, 1), ("mid", 7, 2), ("mid", 10, 2), ("mid", 9, 2), ("mid", 12, 1), ("mid", 11, 2),
+    ("mid", 3, 2), ("mid", 14, 1), ("pmid", 6, 3, 1), ("mid", 13, 1), ("mid", 7, 3), ("mid", 9, 3), ("mid", 5, 2),
+    ("mid", 8, 3), ("pmid", 6, 3, 0), ("mid", 11, 3), ("mid", 10, 3), ("mid", 4, 2), ("mid", 14, 2), ("mid", 12, 2),
+    ("mid", 13, 2), ("pmid", 0, 3, 1), ("mid", 3, 3), ("pmid", 1, 3, 0), ("last", 7), ("last", 9), ("last", 8),
+    ("plast", 6), ("pmid", 1, 3, 1), ("mid", 5, 3), ("last", 11), ("mid", 2, 3), ("last", 10), ("mid", 4, 3),
+    ("mid", 14, 3), ("mid", 12, 3), ("mid", 13, 3), ("last", 5), ("last", 2), ("o_last", 1), ("last", 4),
+    ("plast", 1), ("o_last", 0), ("last", 3), ("o_last", 5), ("o_last", 2), ("last", 14), ("plast", 0), ("o_last", 3),
+    ("last", 12), ("o_last", 4), ("last", 13),
 )
 
 
@@ -284,14 +284,12 @@
 
     def load(i):
         return (
-            pltpu.make_async_copy(gate_hbm.at[:, lanes(i)], gate_buf.at[i], load_sem.at[i]),
-            pltpu.make_async_copy(up_hbm.at[:, lanes(i)], up_buf.at[i], load_sem.at[i]),
+            pltpu.make_async_copy(gate_hbm.at[:, lanes(i)], gate_buf.at[i], load_sem.at[i // LOADS]),
+            pltpu.make_async_copy(up_hbm.at[:, lanes(i)], up_buf.at[i], load_sem.at[i // LOADS]),
         )
 
     def hide():
         def one(i, carry):
-            for copy in load(i):
-                copy.wait()
             gate = gate_buf[i].astype(jnp.float32)
             act = gate / (1.0 + jnp.exp(-gate))
             rows[i, row_block(x), :] = (act * up_buf[i].astype(jnp.float32)).astype(jnp.bfloat16)
@@ -303,7 +301,10 @@
         if PAIRS:
             cols[1, row_block(x), lanes(mine)] = grad_buf[lax.rem(x + 2, NX)]
         with jax.named_scope("hide"):
-            lax.fori_loop(0, CHUNKS, one, 0)
+            for group in range(CHUNKS // LOADS):
+                both = gate_buf.at[pl.ds(0, 2 * LOADS)]
+                pltpu.make_async_copy(both, both, load_sem.at[group]).wait()
+                lax.fori_loop(group * LOADS, (group + 1) * LOADS, one, 0)
 
     partners = (
         at(dz=1), at(dz=-1), at(dz=2), at(dz=-2), at(dx=1), at(dx=-1), at(dx=2), at(dy=1), at(dy=-1), at(dc=1),
@@ -368,7 +369,7 @@
                 pltpu.VMEM((CHUNKS, 7, MC, NB), jnp.bfloat16),
                 pltpu.VMEM((max(PAIRS, 1), MC, NB), jnp.bfloat16),
                 pltpu.VMEM((max(PAIRS, 1), MC, NB), jnp.bfloat16),
-                dma((CHUNKS,)),
+                dma((CHUNKS // LOADS,)),
                 dma,
                 dma,
                 dma((ITEMS, 2)),

time: 77.8 us -> 76.7 us (0.986)
  no operation moved by 1% of the time
where the time goes in v4:
time: 76.7 us; the launch traced here: 76.5 us
  Pallas kernels  75.6 us (99%)
  local copies, waits for them, and re-layouts  0.95 us (1%)
    pallas_call x1, Pallas kernels, shards(): pl.pallas_call(kernel, out_shape=jax.ShapeDtypeStruct((hidden, NB), jnp.f...  75.6 us

profile of v4, /device:TPU:1, one launch (start us, length us, event | category | flops | bytes accessed | tf_op | source)
XLA Modules:
  0.0 76.5 jit_solution(3144744922227214364)
XLA Ops:
  0.0 75.6 %shard_map.37 = f32[1920,128]{1,0:T(8,128)S(1)} custom-call(bf16[448,1920]{1,0:T(8,128)(2,1)} %gate_hbm.1, bf16[448,1920]{1,0:T(8,128)(2,1)} %up_hbm.1, bf16[448,512]{1,0:T(8,128)(2,1)} %grad_hbm.1), custom_call_target="tpu_custom_call" | custom-call | tf_op jit(solution)/shard_map/pallas_call | solution.py:355
  75.6 0.9 %copy.5 = f32[1920,128]{1,0:T(8,128)} copy(f32[1920,128]{1,0:T(8,128)S(1)} %shard_map.37) | data formatting | bytes 1966080

commit v5 on v4

--- a/solution.py
+++ b/solution.py
@@ -23,24 +23,24 @@
     ("b_take", 0, 1), ("x_pass", 1), ("b_pass", 0, 1), ("b_take", 0, 2), ("b_pass", 0, 2), ("x_own", 2),
     ("b_own", 1, 2), ("b_take", 0, 3), ("b_take", 0, 0), ("b_most", 0), ("b_own", 1, 1), ("b_pass", 0, 3),
     ("b_pass", 0, 0), ("x_own", 3), ("part", 0, 0), ("b_far", 0, 1), ("b_far", 0, 2), ("b_take", 1, 2), ("x_pass", 2),
-    ("x_own", 4), ("b_own", 1, 3), ("part", 1, 0), ("b_take", 1, 1), ("pmid", 0, 1, 0), ("b_pass", 1, 2),
-    ("b_far", 0, 0), ("b_pass", 1, 1), ("b_far", 0, 3), ("b_pass", 1, 0), ("x_pass", 3), ("x_pass", 4), ("b_rest", 0),
-    ("part", 1, 1), ("part", 0, 1), ("pmid", 1, 1, 0), ("b_take", 1, 3), ("b_pass", 1, 3), ("x_own", 5),
-    ("pmid", 0, 2, 0), ("product", 2), ("b_most", 1), ("part", 6, 0), ("x_own", 6), ("product", 3), ("pmid", 1, 1, 1),
-    ("b_far", 1, 2), ("pmid", 0, 1, 1), ("pmid", 1, 2, 0), ("b_far", 1, 1), ("b_far", 1, 0), ("product", 4),
-    ("b_far", 1, 3), ("pmid", 0, 3, 0), ("mid", 2, 1), ("x_pass", 5), ("x_own", 7), ("x_own", 8), ("pmid", 6, 1, 0),
-    ("b_rest", 1), ("product", 8), ("x_pass", 6), ("mid", 3, 1), ("product", 7), ("part", 6, 1), ("mid", 4, 1),
-    ("product", 10), ("pmid", 1, 2, 1), ("product", 9), ("mid", 8, 1), ("product", 5), ("x_pass", 7), ("x_pass", 8),
-    ("pmid", 6, 1, 1), ("mid", 2, 2), ("product", 11), ("mid", 10, 1), ("pmid", 0, 2, 1), ("pmid", 6, 2, 0),
-    ("mid", 9, 1), ("mid", 7, 1), ("mid", 5, 1), ("product", 12), ("mid", 11, 1), ("mid", 8, 2), ("product", 14),
-    ("product", 13), ("pmid", 6, 2, 1), ("mid", 7, 2), ("mid", 10, 2), ("mid", 9, 2), ("mid", 12, 1), ("mid", 11, 2),
-    ("mid", 3, 2), ("mid", 14, 1), ("pmid", 6, 3, 1), ("mid", 13, 1), ("mid", 7, 3), ("mid", 9, 3), ("mid", 5, 2),
-    ("mid", 8, 3), ("pmid", 6, 3, 0), ("mid", 11, 3), ("mid", 10, 3), ("mid", 4, 2), ("mid", 14, 2), ("mid", 12, 2),
-    ("mid", 13, 2), ("pmid", 0, 3, 1), ("mid", 3, 3), ("pmid", 1, 3, 0), ("last", 7), ("last", 9), ("last", 8),
-    ("plast", 6), ("pmid", 1, 3, 1), ("mid", 5, 3), ("last", 11), ("mid", 2, 3), ("last", 10), ("mid", 4, 3),
-    ("mid", 14, 3), ("mid", 12, 3), ("mid", 13, 3), ("last", 5), ("last", 2), ("o_last", 1), ("last", 4),
-    ("plast", 1), ("o_last", 0), ("last", 3), ("o_last", 5), ("o_last", 2), ("last", 14), ("plast", 0), ("o_last", 3),
-    ("last", 12), ("o_last", 4), ("last", 13),
+    ("x_own", 4), ("b_own", 1, 3), ("part", 1, 0), ("b_take", 1, 1), ("x_pass", 3), ("pmid", 0, 1, 0),
+    ("b_pass", 1, 2), ("b_far", 0, 0), ("b_pass", 1, 1), ("b_far", 0, 3), ("b_pass", 1, 0), ("x_pass", 4),
+    ("b_rest", 0), ("part", 1, 1), ("part", 0, 1), ("pmid", 1, 1, 0), ("b_take", 1, 3), ("x_own", 5),
+    ("b_pass", 1, 3), ("pmid", 0, 2, 0), ("product", 2), ("b_most", 1), ("part", 6, 0), ("x_own", 6), ("product", 3),
+    ("pmid", 1, 1, 1), ("b_far", 1, 2), ("pmid", 0, 1, 1), ("product", 4), ("pmid", 1, 2, 0), ("b_far", 1, 1),
+    ("b_far", 1, 0), ("b_far", 1, 3), ("mid", 2, 1), ("x_pass", 5), ("x_own", 7), ("x_own", 8), ("pmid", 0, 3, 0),
+    ("pmid", 6, 1, 0), ("b_rest", 1), ("part", 6, 1), ("product", 8), ("x_pass", 6), ("mid", 3, 1), ("product", 7),
+    ("mid", 4, 1), ("product", 10), ("pmid", 1, 2, 1), ("product", 9), ("mid", 8, 1), ("product", 5), ("x_pass", 7),
+    ("x_pass", 8), ("pmid", 6, 1, 1), ("mid", 2, 2), ("product", 11), ("mid", 10, 1), ("pmid", 0, 2, 1),
+    ("pmid", 6, 2, 0), ("mid", 9, 1), ("mid", 7, 1), ("mid", 5, 1), ("product", 12), ("mid", 11, 1), ("mid", 8, 2),
+    ("product", 14), ("product", 13), ("pmid", 6, 2, 1), ("mid", 7, 2), ("mid", 10, 2), ("mid", 9, 2), ("mid", 12, 1),
+    ("mid", 11, 2), ("mid", 3, 2), ("mid", 14, 1), ("pmid", 6, 3, 1), ("mid", 13, 1), ("mid", 7, 3), ("mid", 9, 3),
+    ("mid", 5, 2), ("mid", 8, 3), ("pmid", 6, 3, 0), ("mid", 11, 3), ("mid", 10, 3), ("mid", 4, 2), ("mid", 14, 2),
+    ("mid", 12, 2), ("mid", 13, 2), ("pmid", 0, 3, 1), ("mid", 3, 3), ("pmid", 1, 3, 0), ("last", 7), ("last", 9),
+    ("last", 8), ("plast", 6), ("pmid", 1, 3, 1), ("mid", 5, 3), ("last", 11), ("mid", 2, 3), ("last", 10),
+    ("mid", 4, 3), ("mid", 14, 3), ("mid", 12, 3), ("mid", 13, 3), ("last", 5), ("last", 4), ("last", 2),
+    ("o_last", 1), ("plast", 1), ("o_last", 0), ("last", 3), ("o_last", 5), ("o_last", 2), ("last", 14),
+    ("o_last", 3), ("last", 12), ("o_last", 4), ("plast", 0), ("last", 13),
 )
 
 

time: 76.7 us -> 76.5 us (level)
  no operation moved by 1% of the time
where the time goes in v5:
time: 76.5 us; the launch traced here: 76.4 us
  Pallas kernels  75.4 us (99%)
  local copies, waits for them, and re-layouts  0.95 us (1%)
    pallas_call x1, Pallas kernels, shards(): pl.pallas_call(kernel, out_shape=jax.ShapeDtypeStruct((hidden, NB), jnp.f...  75.4 us

profile of v5, /device:TPU:1, one launch (start us, length us, event | category | flops | bytes accessed | tf_op | source)
XLA Modules:
  0.0 76.4 jit_solution(8700430213652756585)
XLA Ops:
  0.0 75.4 %shard_map.37 = f32[1920,128]{1,0:T(8,128)S(1)} custom-call(bf16[448,1920]{1,0:T(8,128)(2,1)} %gate_hbm.1, bf16[448,1920]{1,0:T(8,128)(2,1)} %up_hbm.1, bf16[448,512]{1,0:T(8,128)(2,1)} %grad_hbm.1), custom_call_target="tpu_custom_call" | custom-call | tf_op jit(solution)/shard_map/pallas_call | solution.py:355
  75.4 0.9 %copy.5 = f32[1920,128]{1,0:T(8,128)} copy(f32[1920,128]{1,0:T(8,128)S(1)} %shard_map.37) | data formatting | bytes 1966080

commit v6 on v5

--- a/solution.py
+++ b/solution.py
@@ -18,9 +18,9 @@
 QUICK = 0
 VMEM_BYTES = 50_000_000
 ORDER = (
-    ("b_near", 0), ("b_own", 0, 0), ("hide",), ("b_own", 1, 0), ("b_far2", 0), ("x_own", 0), ("x_own", 1),
-    ("b_own", 0, 1), ("b_own", 0, 2), ("b_near", 1), ("b_take", 1, 0), ("x_pass", 0), ("b_far2", 1), ("b_own", 0, 3),
-    ("b_take", 0, 1), ("x_pass", 1), ("b_pass", 0, 1), ("b_take", 0, 2), ("b_pass", 0, 2), ("x_own", 2),
+    ("b_near", 0), ("b_own", 0, 0), ("hide",), ("b_own", 1, 0), ("b_far2", 0), ("x_own", 0), ("b_own", 0, 1),
+    ("x_own", 1), ("b_own", 0, 2), ("b_near", 1), ("b_take", 1, 0), ("x_pass", 0), ("b_far2", 1), ("b_own", 0, 3),
+    ("b_take", 0, 1), ("x_pass", 1), ("b_take", 0, 2), ("b_pass", 0, 1), ("b_pass", 0, 2), ("x_own", 2),
     ("b_own", 1, 2), ("b_take", 0, 3), ("b_take", 0, 0), ("b_most", 0), ("b_own", 1, 1), ("b_pass", 0, 3),
     ("b_pass", 0, 0), ("x_own", 3), ("part", 0, 0), ("b_far", 0, 1), ("b_far", 0, 2), ("b_take", 1, 2), ("x_pass", 2),
     ("x_own", 4), ("b_own", 1, 3), ("part", 1, 0), ("b_take", 1, 1), ("x_pass", 3), ("pmid", 0, 1, 0),
@@ -31,15 +31,15 @@
     ("b_far", 1, 0), ("b_far", 1, 3), ("mid", 2, 1), ("x_pass", 5), ("x_own", 7), ("x_own", 8), ("pmid", 0, 3, 0),
     ("pmid", 6, 1, 0), ("b_rest", 1), ("part", 6, 1), ("product", 8), ("x_pass", 6), ("mid", 3, 1), ("product", 7),
     ("mid", 4, 1), ("product", 10), ("pmid", 1, 2, 1), ("product", 9), ("mid", 8, 1), ("product", 5), ("x_pass", 7),
-    ("x_pass", 8), ("pmid", 6, 1, 1), ("mid", 2, 2), ("product", 11), ("mid", 10, 1), ("pmid", 0, 2, 1),
-    ("pmid", 6, 2, 0), ("mid", 9, 1), ("mid", 7, 1), ("mid", 5, 1), ("product", 12), ("mid", 11, 1), ("mid", 8, 2),
-    ("product", 14), ("product", 13), ("pmid", 6, 2, 1), ("mid", 7, 2), ("mid", 10, 2), ("mid", 9, 2), ("mid", 12, 1),
-    ("mid", 11, 2), ("mid", 3, 2), ("mid", 14, 1), ("pmid", 6, 3, 1), ("mid", 13, 1), ("mid", 7, 3), ("mid", 9, 3),
-    ("mid", 5, 2), ("mid", 8, 3), ("pmid", 6, 3, 0), ("mid", 11, 3), ("mid", 10, 3), ("mid", 4, 2), ("mid", 14, 2),
-    ("mid", 12, 2), ("mid", 13, 2), ("pmid", 0, 3, 1), ("mid", 3, 3), ("pmid", 1, 3, 0), ("last", 7), ("last", 9),
-    ("last", 8), ("plast", 6), ("pmid", 1, 3, 1), ("mid", 5, 3), ("last", 11), ("mid", 2, 3), ("last", 10),
-    ("mid", 4, 3), ("mid", 14, 3), ("mid", 12, 3), ("mid", 13, 3), ("last", 5), ("last", 4), ("last", 2),
-    ("o_last", 1), ("plast", 1), ("o_last", 0), ("last", 3), ("o_last", 5), ("o_last", 2), ("last", 14),
+    ("x_pass", 8), ("mid", 2, 2), ("mid", 10, 1), ("product", 11), ("pmid", 0, 2, 1), ("pmid", 6, 2, 0),
+    ("mid", 9, 1), ("mid", 7, 1), ("mid", 5, 1), ("pmid", 6, 1, 1), ("product", 12), ("mid", 11, 1), ("mid", 8, 2),
+    ("product", 14), ("product", 13), ("mid", 7, 2), ("pmid", 6, 2, 1), ("mid", 10, 2), ("mid", 9, 2), ("mid", 12, 1),
+    ("mid", 11, 2), ("pmid", 0, 3, 1), ("mid", 3, 2), ("mid", 14, 1), ("pmid", 6, 3, 1), ("mid", 13, 1),
+    ("mid", 7, 3), ("mid", 9, 3), ("mid", 5, 2), ("mid", 8, 3), ("pmid", 6, 3, 0), ("mid", 10, 3), ("mid", 11, 3),
+    ("mid", 4, 2), ("mid", 14, 2), ("mid", 12, 2), ("mid", 13, 2), ("mid", 3, 3), ("pmid", 1, 3, 0), ("last", 7),
+    ("last", 9), ("last", 8), ("plast", 6), ("pmid", 1, 3, 1), ("mid", 5, 3), ("last", 11), ("mid", 2, 3),
+    ("last", 10), ("mid", 4, 3), ("mid", 14, 3), ("mid", 12, 3), ("mid", 13, 3), ("last", 5), ("last", 4),
+    ("last", 2), ("o_last", 1), ("plast", 1), ("o_last", 0), ("last", 3), ("o_last", 5), ("o_last", 2), ("last", 14),
     ("o_last", 3), ("last", 12), ("o_last", 4), ("plast", 0), ("last", 13),
 )
 
@@ -307,8 +307,10 @@
                 lax.fori_loop(group * LOADS, (group + 1) * LOADS, one, 0)
 
     partners = (
-        at(dz=1), at(dz=-1), at(dz=2), at(dz=-2), at(dx=1), at(dx=-1), at(dx=2), at(dy=1), at(dy=-1), at(dc=1),
+        at(dz=1), at(dz=-1), at(dx=1), at(dx=-1), at(dx=2), at(dy=1), at(dy=-1), at(dc=1),
     )
+    if QUICK:
+        partners += (at(dz=2), at(dz=-2))
     barrier = pltpu.get_barrier_semaphore()
     for device in partners:
         pl.semaphore_signal(barrier, inc=1, device_id=device, device_id_type=MESH)

time: 76.5 us -> 76.4 us (level)
  no operation moved by 1% of the time
where the time goes in v6:
time: 76.4 us; the launch traced here: 76.3 us
  Pallas kernels  75.3 us (99%)
  local copies, waits for them, and re-layouts  0.95 us (1%)
    pallas_call x1, Pallas kernels, shards(): pl.pallas_call(kernel, out_shape=jax.ShapeDtypeStruct((hidden, NB), jnp.f...  75.3 us

profile of v6, /device:TPU:1, one launch (start us, length us, event | category | flops | bytes accessed | tf_op | source)
XLA Modules:
  0.0 76.3 jit_solution(2325681863622660538)
XLA Ops:
  0.0 75.3 %shard_map.37 = f32[1920,128]{1,0:T(8,128)S(1)} custom-call(bf16[448,1920]{1,0:T(8,128)(2,1)} %gate_hbm.1, bf16[448,1920]{1,0:T(8,128)(2,1)} %up_hbm.1, bf16[448,512]{1,0:T(8,128)(2,1)} %grad_hbm.1), custom_call_target="tpu_custom_call" | custom-call | tf_op jit(solution)/shard_map/pallas_call | solution.py:357
  75.3 0.9 %copy.5 = f32[1920,128]{1,0:T(8,128)} copy(f32[1920,128]{1,0:T(8,128)S(1)} %shard_map.37) | data formatting | bytes 1966080

commit v7 on v6

--- a/solution.py
+++ b/solution.py
@@ -18,7 +18,7 @@
 QUICK = 0
 VMEM_BYTES = 50_000_000
 ORDER = (
-    ("b_near", 0), ("b_own", 0, 0), ("hide",), ("b_own", 1, 0), ("b_far2", 0), ("x_own", 0), ("b_own", 0, 1),
+    ("b_near", 0), ("b_own", 0, 0), ("b_own", 1, 0), ("hide",), ("b_far2", 0), ("x_own", 0), ("b_own", 0, 1),
     ("x_own", 1), ("b_own", 0, 2), ("b_near", 1), ("b_take", 1, 0), ("x_pass", 0), ("b_far2", 1), ("b_own", 0, 3),
     ("b_take", 0, 1), ("x_pass", 1), ("b_take", 0, 2), ("b_pass", 0, 1), ("b_pass", 0, 2), ("x_own", 2),
     ("b_own", 1, 2), ("b_take", 0, 3), ("b_take", 0, 0), ("b_most", 0), ("b_own", 1, 1), ("b_pass", 0, 3),
@@ -95,19 +95,22 @@
     def b_far2(n):
         b_send_to(n, 2, 2)
 
-    def b_along(n, k, block, sem, dy):
-        remote(piece(n, k, block), piece(n, k, block), b_send.at[1], sem, at(dy=dy)).start()
-
-    def b_over(n, k, block, part=0):
-        remote(piece(n, k, block), piece(n, k, block), b_send.at[2], bs_recv.at[n, part], at(dc=1)).start()
+    def held(n, k, block, own):
+        return grad_buf.at[lax.rem(x + 2 * n, NX)] if own and k == 0 else piece(n, k, block)
+
+    def b_along(n, k, block, sem, dy, own=False):
+        remote(held(n, k, block, own), piece(n, k, block), b_send.at[1], sem, at(dy=dy)).start()
+
+    def b_over(n, k, block, part=0, own=False):
+        remote(held(n, k, block, own), piece(n, k, block), b_send.at[2], bs_recv.at[n, part], at(dc=1)).start()
 
     def b_own(n, k):
         if k:
             with jax.named_scope(f"bx_{n}{k}"):
                 arrived(grad_buf.at[0], bx_recv.at[n, k - 1])
-        b_along(n, k, mine, by_recv.at[n, k, 0], 1)
-        b_along(n, k, mine, by_recv.at[n, k, 0], -1)
-        b_over(n, k, mine)
+        b_along(n, k, mine, by_recv.at[n, k, 0], 1, own=True)
+        b_along(n, k, mine, by_recv.at[n, k, 0], -1, own=True)
+        b_over(n, k, mine, own=True)
 
     def b_take(n, k):
         with jax.named_scope(f"by_{n}{k}"):
@@ -298,8 +301,8 @@
         for i in range(CHUNKS):
             for copy in load(i):
                 copy.start()
-        if PAIRS:
-            cols[1, row_block(x), lanes(mine)] = grad_buf[lax.rem(x + 2, NX)]
+        for n in range(2 if PAIRS else 1):
+            cols[n, row_block(x), lanes(mine)] = grad_buf[lax.rem(x + 2 * n, NX)]
         with jax.named_scope("hide"):
             for group in range(CHUNKS // LOADS):
                 both = gate_buf.at[pl.ds(0, 2 * LOADS)]
@@ -321,7 +324,6 @@
         copy.start()
     with jax.named_scope("grad"):
         pltpu.make_async_copy(grad_buf, grad_buf, grad_sem).wait()
-    cols[0, row_block(x), lanes(mine)] = grad_buf[x]
     with jax.named_scope("barrier"):
         pl.semaphore_wait(barrier, len(partners))
 

time: 76.4 us -> 76.4 us (level)
  no operation moved by 1% of the time
where the time goes in v7:
time: 76.4 us; the launch traced here: 76.3 us
  Pallas kernels  75.3 us (99%)
  local copies, waits for them, and re-layouts  0.95 us (1%)
    pallas_call x1, Pallas kernels, shards(): pl.pallas_call(kernel, out_shape=jax.ShapeDtypeStruct((hidden, NB), jnp.f...  75.3 us

profile of v7, /device:TPU:1, one launch (start us, length us, event | category | flops | bytes accessed | tf_op | source)
XLA Modules:
  0.0 76.3 jit_solution(15094118564264215363)
XLA Ops:
  0.0 75.3 %shard_map.37 = f32[1920,128]{1,0:T(8,128)S(1)} custom-call(bf16[448,1920]{1,0:T(8,128)(2,1)} %gate_hbm.1, bf16[448,1920]{1,0:T(8,128)(2,1)} %up_hbm.1, bf16[448,512]{1,0:T(8,128)(2,1)} %grad_hbm.1), custom_call_target="tpu_custom_call" | custom-call | tf_op jit(solution)/shard_map/pallas_call | solution.py:359
  75.3 0.9 %copy.5 = f32[1920,128]{1,0:T(8,128)} copy(f32[1920,128]{1,0:T(8,128)S(1)} %shard_map.37) | data formatting | bytes 1966080

commit v8 on v7

--- a/solution.py
+++ b/solution.py
@@ -8,7 +8,7 @@
 MESH = pl.DeviceIdType.MESH
 NZ, NX, NY, NC = 8, 4, 4, 2
 MC = 128
-LOADS = 5
+LOADS = 3
 NB = 128
 CHUNKS = 15
 PAIRS = 6

time: 76.4 us -> 76.2 us (level)
  no operation moved by 1% of the time
where the time goes in v8:
time: 76.2 us; the launch traced here: 76.1 us
  Pallas kernels  75.2 us (99%)
  local copies, waits for them, and re-layouts  0.95 us (1%)
    pallas_call x1, Pallas kernels, shards(): pl.pallas_call(kernel, out_shape=jax.ShapeDtypeStruct((hidden, NB), jnp.f...  75.2 us

profile of v8, /device:TPU:1, one launch (start us, length us, event | category | flops | bytes accessed | tf_op | source)
XLA Modules:
  0.0 76.1 jit_solution(13255956384087515713)
XLA Ops:
  0.0 75.2 %shard_map.37 = f32[1920,128]{1,0:T(8,128)S(1)} custom-call(bf16[448,1920]{1,0:T(8,128)(2,1)} %gate_hbm.1, bf16[448,1920]{1,0:T(8,128)(2,1)} %up_hbm.1, bf16[448,512]{1,0:T(8,128)(2,1)} %grad_hbm.1), custom_call_target="tpu_custom_call" | custom-call | tf_op jit(solution)/shard_map/pallas_call | solution.py:359
  75.2 0.9 %copy.5 = f32[1920,128]{1,0:T(8,128)} copy(f32[1920,128]{1,0:T(8,128)S(1)} %shard_map.37) | data formatting | bytes 1966080
